TPU v7x, 128 devices: a whole 4x4x4 slice. The times are simulated.
128 devices in a mesh: rows: 2 (over y_hi), cols: 8 (over z, y_lo), slabs: 8 (over x, core).
Axes of the slice: x: 4, y: 4 (y_hi: 2, y_lo: 2; y = y_hi * 2 + y_lo), z: 4, core: 2. Of those that a mesh axis runs over, the one named last changes fastest.
Arguments:
- field_values: float32 [8, 512, 512, 128], P('rows', 'cols', 'slabs'), may hold values from 0.2 to 1.8
- mobility: float32 [8, 512, 512, 128], P('rows', 'cols', 'slabs'), may hold values from 0.03 to 0.15
- source: float32 [8, 512, 512, 128], P('rows', 'cols', 'slabs'), may hold values from -0.2 to 0.2
Outputs:
- column_sum: float32 [8, 512, 512, 128], P('rows', 'cols', 'slabs')
- field_values_end: float32 [8, 512, 512, 128], P('rows', 'cols', 'slabs')
All inputs are finite; a program needn't handle non-finite values.
Results may differ from a plain program's by a relative error of at most 0.00002.
Values sent between devices are 32-bit elements; how exact they have to be, the bound alone decides.
A program may use at most 320 MiB of HBM per device.

v0:
```python
import jax
import jax.numpy as jnp
from jax import lax
from jax.sharding import PartitionSpec as P

STEPS = 4


def extended(array, sides, width):
    edges = {}
    for axis, dim in sides:
        count, length = (lax.axis_size(axis), array.shape[dim])
        up = [(i, (i + 1) % count) for i in range(count - 1)]
        last = lax.slice_in_dim(array, length - width, length, axis=dim)
        first = lax.slice_in_dim(array, 0, width, axis=dim)
        edges[dim] = (
            lax.ppermute(last, axis, up),
            lax.ppermute(first, axis, [(b, a) for a, b in up]),
        )
    done = []
    for _, dim in sides:
        low, high = edges[dim]
        around = [(width, width) if d in done else (0, 0) for d in range(array.ndim)]
        array = jnp.concatenate([jnp.pad(low, around), array, jnp.pad(high, around)], axis=dim)
        done.append(dim)
    return array


def sent_to_all(array, axis):
    count = lax.axis_size(axis)
    return lax.all_to_all(
        jnp.broadcast_to(array[None], (count, *array.shape)), axis, 0, 0, tiled=True
    )


def folded_in_pairs(pieces, combine):
    while len(jax.tree.leaves(pieces)[0]) > 1:
        pieces = jax.vmap(combine)(*(pieces[side::2] for side in (0, 1)))
    return pieces[0]


def carried_in(array, axis, combine, identity):
    count, index = (lax.axis_size(axis), lax.axis_index(axis))
    passed = jnp.arange(count) < index

    def kept(part, zero, own):
        part = jnp.where(
            passed.reshape(-1, *(1 for _ in own.shape)), part, jnp.asarray(zero, own.dtype)
        )
        return part

    pieces = sent_to_all(array, axis)
    return folded_in_pairs(kept(pieces, identity, array), combine)


def strip_edges(values, dims):
    for dim in dims:
        values = lax.slice_in_dim(values, 1, values.shape[dim] - 1, axis=dim)
    return values


def neighbour(values, dim, start, dims):
    others = [other for other in dims if other != dim]
    values = strip_edges(values, others)
    return lax.slice_in_dim(values, start, start + values.shape[dim] - 2, axis=dim)


def one_step(padded, mobility, source):
    middle = strip_edges(padded, (0, 1, 2))
    lower = [neighbour(padded, dim, 0, (0, 1, 2)) for dim in (0, 1, 2)]
    upper = [neighbour(padded, dim, 2, (0, 1, 2)) for dim in (0, 1, 2)]
    spread = lower[0] + upper[0] + lower[1] + upper[1] + lower[2] + upper[2] - 6.0 * middle
    return middle + mobility * spread + source


def local(field_values, mobility, source):
    for step in range(STEPS):
        padded = extended(field_values, (("rows", 0), ("cols", 1), ("slabs", 2)), 1)
        field_values = one_step(padded, mobility, source)
    here = jnp.cumsum(field_values, axis=0)
    total = lax.slice_in_dim(here, here.shape[0] - 1, here.shape[0], axis=0)

    def add_pair(earlier_total, later_total):
        return earlier_total + later_total

    below = carried_in(total, "rows", add_pair, jnp.zeros_like(total))
    column_sum = (here + below) / (field_values.shape[0] * lax.axis_size("rows"))
    return (column_sum, field_values)


def solution(mesh):
    in_specs = (
        P("rows", "cols", "slabs", None),
        P("rows", "cols", "slabs", None),
        P("rows", "cols", "slabs", None),
    )
    out_specs = (P("rows", "cols", "slabs", None), P("rows", "cols", "slabs", None))
    return jax.shard_map(local, mesh=mesh, in_specs=in_specs, out_specs=out_specs, check_vma=False)
```

profile of v0, /device:TPU:112, one launch (start us, length us, event | category | flops | bytes accessed | tf_op | source)
XLA Modules:
  0.0 452.1 jit_solution(7750534478129803288)
XLA Ops:
  0.6 4.1 fusion.56
  6.2 6.3 %collective-permute-start.1 = (f32[1,64,64,128]{3,2,1,0:T(8,128)}, f32[1,64,64,128]{3,2,1,0:T(8,128)S(1)}, u32[]{:S(2)}, u32[]{:S(2)}) collective-permute-start(f32[1,64,64,128]{3,2,1,0:T(8,128)} %get-tuple-element.26), channel_id=1, source_target_pairs={{64,0},{65,1},{66,2},{67,3},{68,4},{69,5},{70,6},{71,7},{72,8},{73... | collective-permute-start | bytes 6291464 | tf_op jit(solution)/shard_map/ppermute | solution.py:18
  15.8 3.6 collective-permute-start.3
  20.8 42.2 %collective-permute-done.2 = f32[4,1,64,128]{3,2,1,0:T(8,128)S(1)} collective-permute-done((f32[4,1,64,128]{3,2,1,0:T(8,128)S(1)}, f32[4,1,64,128]{3,2,1,0:T(8,128)S(1)}, u32[]{:S(2)}, u32[]{:S(2)}) %collective-permute-start.2) | collective-permute-done | bytes 131104 | tf_op jit(solution)/shard_map/ppermute | solution.py:17
  65.8 4.7 %constant_dynamic-update-slice_fusion.1 = f32[6,64,64,128]{3,2,1,0:T(8,128)} fusion(f32[6,64,64,128]{3,2,1,0:T(8,128)} %constant_dynamic-update-slice_fusion.2, f32[4,64,64,128]{3,2,1,0:T(8,128)S(1)} %copy-done), kind=kLoop, calls=%fused_computation.116 | loop fusion | bytes 16777216
  73.4 26.0 %fusion.38 = f32[4,64,64,128]{3,2,1,0:T(8,128)} fusion(f32[4,64,64,128]{3,2,1,0:T(8,128)S(1)} %bitcast.22, f32[4,64,64,128]{3,2,1,0:T(8,128)} %param.3, f32[4,64,64,128]{3,2,1,0:T(8,128)} %param.4, f32[4,64,1,128]{3,2,1,0:T(1,128)S(1)} %bitcast.27, f32[6,1,64,128]{3,2,1,0:T(8,128)S(1)} %pad.51, f32[6,64,64,128]{3,2,1,0:T(8,128)} %constant_dynamic-update-slice_fusion, ...), kind=kLoop, calls=%fused_computation.93 | loop fusion | flops 54525952 | bytes 50987008 | tf_op jit(solution)/shard_map/add | solution.py:73
  103.2 7.5 %collective-permute-start.7 = (f32[1,64,64,128]{3,2,1,0:T(8,128)S(1)}, f32[1,64,64,128]{3,2,1,0:T(8,128)}, u32[]{:S(2)}, u32[]{:S(2)}) collective-permute-start(f32[1,64,64,128]{3,2,1,0:T(8,128)S(1)} %get-tuple-element.19), channel_id=1, source_target_pairs={{64,0},{65,1},{66,2},{67,3},{68,4},{69,5},{70,6},{71,7},{72,8},{73... | collective-permute-start | bytes 6291464 | tf_op jit(solution)/shard_map/ppermute | solution.py:18
  114.5 3.9 collective-permute-start.9
  122.1 38.4 %collective-permute-done.8 = f32[4,1,64,128]{3,2,1,0:T(8,128)S(1)} collective-permute-done((f32[4,1,64,128]{3,2,1,0:T(8,128)S(1)}, f32[4,1,64,128]{3,2,1,0:T(8,128)S(1)}, u32[]{:S(2)}, u32[]{:S(2)}) %collective-permute-start.8) | collective-permute-done | bytes 131104 | tf_op jit(solution)/shard_map/ppermute | solution.py:17
  163.7 28.3 %fusion.27 = f32[4,64,64,128]{3,2,1,0:T(8,128)} fusion(f32[4,64,64,128]{3,2,1,0:T(8,128)} %param.5, f32[4,64,64,128]{3,2,1,0:T(8,128)} %fusion.38, f32[4,64,64,128]{3,2,1,0:T(8,128)} %param.4, f32[4,64,1,128]{3,2,1,0:T(1,128)S(1)} %bitcast.29, f32[6,1,64,128]{3,2,1,0:T(8,128)S(1)} %pad.55, f32[6,1,64,128]{3,2,1,0:T(8,128)S(1)} %pad.54, ...), kind=kLoop, calls=%fused_computation.64 | loop fusion | flops 71303168 | bytes 38404096 | tf_op jit(solution)/shard_map/add | solution.py:73
  195.8 7.5 %collective-permute-start.13 = (f32[1,64,64,128]{3,2,1,0:T(8,128)S(1)}, f32[1,64,64,128]{3,2,1,0:T(8,128)}, u32[]{:S(2)}, u32[]{:S(2)}) collective-permute-start(f32[1,64,64,128]{3,2,1,0:T(8,128)S(1)} %get-tuple-element.13), channel_id=1, source_target_pairs={{64,0},{65,1},{66,2},{67,3},{68,4},{69,5},{70,6},{71,7},{72,8},{73... | collective-permute-start | bytes 6291464 | tf_op jit(solution)/shard_map/ppermute | solution.py:18
  206.4 4.7 %collective-permute-start.15 = (f32[4,1,64,128]{3,2,1,0:T(8,128)S(1)}, f32[4,1,64,128]{3,2,1,0:T(8,128)S(1)}, u32[]{:S(2)}, u32[]{:S(2)}) collective-permute-start(f32[4,1,64,128]{3,2,1,0:T(8,128)S(1)} %get-tuple-element.15), channel_id=1, source_target_pairs={{8,0},{16,8},{24,16},{32,24},{40,32},{48,40},{56,48},{9,1},{17,9},... | collective-permute-start | bytes 393224 | tf_op jit(solution)/shard_map/ppermute | solution.py:18
  212.9 3.7 collective-permute-start.16
  216.6 33.8 %collective-permute-done.14 = f32[4,1,64,128]{3,2,1,0:T(8,128)S(1)} collective-permute-done((f32[4,1,64,128]{3,2,1,0:T(8,128)S(1)}, f32[4,1,64,128]{3,2,1,0:T(8,128)S(1)}, u32[]{:S(2)}, u32[]{:S(2)}) %collective-permute-start.14) | collective-permute-done | bytes 131104 | tf_op jit(solution)/shard_map/ppermute | solution.py:17
  252.0 3.8 collective-permute-done.17
  255.8 28.3 %fusion.16 = f32[4,64,64,128]{3,2,1,0:T(8,128)} fusion(f32[4,64,64,128]{3,2,1,0:T(8,128)} %param.5, f32[4,64,64,128]{3,2,1,0:T(8,128)} %fusion.27, f32[4,64,64,128]{3,2,1,0:T(8,128)} %param.4, f32[4,64,1,128]{3,2,1,0:T(1,128)S(1)} %bitcast.30, f32[6,1,64,128]{3,2,1,0:T(8,128)S(1)} %pad.59, f32[6,1,64,128]{3,2,1,0:T(8,128)S(1)} %pad.58, ...), kind=kLoop, calls=%fused_computation.35 | loop fusion | flops 71303168 | bytes 38404096 | tf_op jit(solution)/shard_map/add | solution.py:73
  287.9 7.5 %collective-permute-start.19 = (f32[1,64,64,128]{3,2,1,0:T(8,128)S(1)}, f32[1,64,64,128]{3,2,1,0:T(8,128)}, u32[]{:S(2)}, u32[]{:S(2)}) collective-permute-start(f32[1,64,64,128]{3,2,1,0:T(8,128)S(1)} %get-tuple-element.7), channel_id=1, source_target_pairs={{64,0},{65,1},{66,2},{67,3},{68,4},{69,5},{70,6},{71,7},{72,8},{73... | collective-permute-start | bytes 6291464 | tf_op jit(solution)/shard_map/ppermute | solution.py:18
  306.3 36.3 %collective-permute-done.20 = f32[4,1,64,128]{3,2,1,0:T(8,128)S(1)} collective-permute-done((f32[4,1,64,128]{3,2,1,0:T(8,128)S(1)}, f32[4,1,64,128]{3,2,1,0:T(8,128)S(1)}, u32[]{:S(2)}, u32[]{:S(2)}) %collective-permute-start.20) | collective-permute-done | bytes 131104 | tf_op jit(solution)/shard_map/ppermute | solution.py:17
  342.5 5.4 %collective-permute-start.22 = (f32[4,64,1,128]{3,1,2,0:T(8,128)S(1)}, f32[4,64,1,128]{3,1,2,0:T(8,128)S(1)}, u32[]{:S(2)}, u32[]{:S(2)}) collective-permute-start(f32[4,64,1,128]{3,1,2,0:T(8,128)S(1)} %bitcast.33), channel_id=1, source_target_pairs={{0,1},{1,2},{2,3},{3,4},{4,5},{5,6},{6,7},{8,9},{9,10},{10,11},{11... | collective-permute-start | bytes 393224 | tf_op jit(solution)/shard_map/ppermute | solution.py:17
  348.9 28.3 %fusion.5 = f32[4,64,64,128]{3,2,1,0:T(8,128)} fusion(f32[4,64,64,128]{3,2,1,0:T(8,128)} %param.5, f32[4,64,64,128]{3,2,1,0:T(8,128)} %fusion.16, f32[4,64,64,128]{3,2,1,0:T(8,128)} %param.4, f32[4,64,1,128]{3,2,1,0:T(1,128)S(1)} %bitcast.24, f32[6,1,64,128]{3,2,1,0:T(8,128)S(1)} %pad.63, f32[6,1,64,128]{3,2,1,0:T(8,128)S(1)} %pad.62, ...), kind=kLoop, calls=%fused_computation.6 | loop fusion | flops 71303168 | bytes 38404096 | tf_op jit(solution)/shard_map/add | solution.py:73
  377.2 8.7 %fusion.57 = f32[4,64,64,128]{3,2,1,0:T(8,128)} fusion(f32[4,64,64,128]{3,2,1,0:T(8,128)} %fusion.5), kind=kOutput, calls=%fused_computation.131 | output fusion | flops 6291456 | bytes 16777216 | tf_op jit(solution)/shard_map/jit(cumsum)/reduce_window_sum | solution.py:80
  390.3 5.6 %all-to-all-start = ((f32[2,1,64,64,128]{4,3,2,1,0:T(8,128)}), f32[2,1,64,64,128]{4,3,2,1,0:T(8,128)}, u32[]{:S(2)}, u32[]{:S(2)}) async-start(f32[2,1,64,64,128]{4,3,2,1,0:T(8,128)} %broadcast_in_dim.23), calls=%async_computation | async-start | bytes 8388608 | tf_op jit(solution)/shard_map/all_to_all | solution.py:31
  395.9 44.3 %all-to-all-done = f32[2,1,64,64,128]{4,3,2,1,0:T(8,128)} async-done(((f32[2,1,64,64,128]{4,3,2,1,0:T(8,128)}), f32[2,1,64,64,128]{4,3,2,1,0:T(8,128)}, u32[]{:S(2)}, u32[]{:S(2)}) %all-to-all-start) | async-done | bytes 4194336 | tf_op jit(solution)/shard_map/all_to_all | solution.py:31
  443.3 8.8 %add_multiply_fusion = f32[4,64,64,128]{3,2,1,0:T(8,128)} fusion(f32[4,64,64,128]{3,2,1,0:T(8,128)} %fusion.57, f32[64,64,128]{2,1,0:T(8,128)S(1)} %fusion.44), kind=kLoop, calls=%fused_computation.110 | loop fusion | flops 4194304 | bytes 18874368 | tf_op jit(solution)/shard_map/div | solution.py:87
  (69 shorter events, 59.4 us)
Async XLA Ops:
  4.8 59.5 %collective-permute-start = (f32[1,64,64,128]{3,2,1,0:T(8,128)S(1)}, f32[1,64,64,128]{3,2,1,0:T(8,128)S(1)}, u32[]{:S(2)}, u32[]{:S(2)}) collective-permute-start(f32[1,64,64,128]{3,2,1,0:T(8,128)S(1)} %get-tuple-element.27), channel_id=1, source_target_pairs={{0,64},{1,65},{2,66},{3,67},{4,68},{5,69},{6,70},{7,71},{8,72},{9,... | collective-permute-start | bytes 6291464 | tf_op jit(solution)/shard_map/ppermute | solution.py:17
  6.2 64.3 %collective-permute-start.1 = (f32[1,64,64,128]{3,2,1,0:T(8,128)}, f32[1,64,64,128]{3,2,1,0:T(8,128)S(1)}, u32[]{:S(2)}, u32[]{:S(2)}) collective-permute-start(f32[1,64,64,128]{3,2,1,0:T(8,128)} %get-tuple-element.26), channel_id=1, source_target_pairs={{64,0},{65,1},{66,2},{67,3},{68,4},{69,5},{70,6},{71,7},{72,8},{73... | collective-permute-start | bytes 6291464 | tf_op jit(solution)/shard_map/ppermute | solution.py:18
  12.6 50.4 %collective-permute-start.2 = (f32[4,1,64,128]{3,2,1,0:T(8,128)S(1)}, f32[4,1,64,128]{3,2,1,0:T(8,128)S(1)}, u32[]{:S(2)}, u32[]{:S(2)}) collective-permute-start(f32[4,1,64,128]{3,2,1,0:T(8,128)S(1)} %get-tuple-element.24), channel_id=1, source_target_pairs={{0,8},{8,16},{16,24},{24,32},{32,40},{40,48},{48,56},{1,9},{9,17},... | collective-permute-start | bytes 393224 | tf_op jit(solution)/shard_map/ppermute | solution.py:17
  15.8 48.5 %collective-permute-start.3 = (f32[4,1,64,128]{3,2,1,0:T(8,128)S(1)}, f32[4,1,64,128]{3,2,1,0:T(8,128)S(1)}, u32[]{:S(2)}, u32[]{:S(2)}) collective-permute-start(f32[4,1,64,128]{3,2,1,0:T(8,128)S(1)} %get-tuple-element.25), channel_id=1, source_target_pairs={{8,0},{16,8},{24,16},{32,24},{40,32},{48,40},{56,48},{9,1},{17,9},... | collective-permute-start | bytes 393224 | tf_op jit(solution)/shard_map/ppermute | solution.py:18
  19.5 53.8 %collective-permute-start.4 = (f32[4,64,1,128]{3,1,2,0:T(8,128)S(1)}, f32[4,64,1,128]{3,1,2,0:T(8,128)S(1)}, u32[]{:S(2)}, u32[]{:S(2)}) collective-permute-start(f32[4,64,1,128]{3,1,2,0:T(8,128)S(1)} %bitcast.32), channel_id=1, source_target_pairs={{0,1},{1,2},{2,3},{3,4},{4,5},{5,6},{6,7},{8,9},{9,10},{10,11},{11... | collective-permute-start | bytes 393224 | tf_op jit(solution)/shard_map/ppermute | solution.py:17
  63.0 10.4 %collective-permute-start.5 = (f32[4,64,1,128]{3,1,2,0:T(8,128)S(1)}, f32[4,64,1,128]{3,1,2,0:T(8,128)S(1)}, u32[]{:S(2)}, u32[]{:S(2)}) collective-permute-start(f32[4,64,1,128]{3,1,2,0:T(8,128)S(1)} %bitcast.31), channel_id=1, source_target_pairs={{1,0},{2,1},{3,2},{4,3},{5,4},{6,5},{7,6},{9,8},{10,9},{11,10},{12... | collective-permute-start | bytes 393224 | tf_op jit(solution)/shard_map/ppermute | solution.py:18
  101.9 61.9 %collective-permute-start.6 = (f32[1,64,64,128]{3,2,1,0:T(8,128)S(1)}, f32[1,64,64,128]{3,2,1,0:T(8,128)S(1)}, u32[]{:S(2)}, u32[]{:S(2)}) collective-permute-start(f32[1,64,64,128]{3,2,1,0:T(8,128)S(1)} %get-tuple-element.18), channel_id=1, source_target_pairs={{0,64},{1,65},{2,66},{3,67},{4,68},{5,69},{6,70},{7,71},{8,72},{9,... | collective-permute-start | bytes 6291464 | tf_op jit(solution)/shard_map/ppermute | solution.py:17
  103.2 60.6 %collective-permute-start.7 = (f32[1,64,64,128]{3,2,1,0:T(8,128)S(1)}, f32[1,64,64,128]{3,2,1,0:T(8,128)}, u32[]{:S(2)}, u32[]{:S(2)}) collective-permute-start(f32[1,64,64,128]{3,2,1,0:T(8,128)S(1)} %get-tuple-element.19), channel_id=1, source_target_pairs={{64,0},{65,1},{66,2},{67,3},{68,4},{69,5},{70,6},{71,7},{72,8},{73... | collective-permute-start | bytes 6291464 | tf_op jit(solution)/shard_map/ppermute | solution.py:18
  111.7 48.8 %collective-permute-start.8 = (f32[4,1,64,128]{3,2,1,0:T(8,128)S(1)}, f32[4,1,64,128]{3,2,1,0:T(8,128)S(1)}, u32[]{:S(2)}, u32[]{:S(2)}) collective-permute-start(f32[4,1,64,128]{3,2,1,0:T(8,128)S(1)} %get-tuple-element.20), channel_id=1, source_target_pairs={{0,8},{8,16},{16,24},{24,32},{32,40},{40,48},{48,56},{1,9},{9,17},... | collective-permute-start | bytes 393224 | tf_op jit(solution)/shard_map/ppermute | solution.py:17
  114.5 47.3 %collective-permute-start.9 = (f32[4,1,64,128]{3,2,1,0:T(8,128)S(1)}, f32[4,1,64,128]{3,2,1,0:T(8,128)S(1)}, u32[]{:S(2)}, u32[]{:S(2)}) collective-permute-start(f32[4,1,64,128]{3,2,1,0:T(8,128)S(1)} %get-tuple-element.21), channel_id=1, source_target_pairs={{8,0},{16,8},{24,16},{32,24},{40,32},{48,40},{56,48},{9,1},{17,9},... | collective-permute-start | bytes 393224 | tf_op jit(solution)/shard_map/ppermute | solution.py:18
  120.2 41.6 %collective-permute-start.10 = (f32[4,64,1,128]{3,1,2,0:T(8,128)S(1)}, f32[4,64,1,128]{3,1,2,0:T(8,128)S(1)}, u32[]{:S(2)}, u32[]{:S(2)}) collective-permute-start(f32[4,64,1,128]{3,1,2,0:T(8,128)S(1)} %bitcast.37), channel_id=1, source_target_pairs={{0,1},{1,2},{2,3},{3,4},{4,5},{5,6},{6,7},{8,9},{9,10},{10,11},{11... | collective-permute-start | bytes 393224 | tf_op jit(solution)/shard_map/ppermute | solution.py:17
  194.5 61.3 %collective-permute-start.12 = (f32[1,64,64,128]{3,2,1,0:T(8,128)S(1)}, f32[1,64,64,128]{3,2,1,0:T(8,128)S(1)}, u32[]{:S(2)}, u32[]{:S(2)}) collective-permute-start(f32[1,64,64,128]{3,2,1,0:T(8,128)S(1)} %get-tuple-element.12), channel_id=1, source_target_pairs={{0,64},{1,65},{2,66},{3,67},{4,68},{5,69},{6,70},{7,71},{8,72},{9,... | collective-permute-start | bytes 6291464 | tf_op jit(solution)/shard_map/ppermute | solution.py:17
  195.8 60.0 %collective-permute-start.13 = (f32[1,64,64,128]{3,2,1,0:T(8,128)S(1)}, f32[1,64,64,128]{3,2,1,0:T(8,128)}, u32[]{:S(2)}, u32[]{:S(2)}) collective-permute-start(f32[1,64,64,128]{3,2,1,0:T(8,128)S(1)} %get-tuple-element.13), channel_id=1, source_target_pairs={{64,0},{65,1},{66,2},{67,3},{68,4},{69,5},{70,6},{71,7},{72,8},{73... | collective-permute-start | bytes 6291464 | tf_op jit(solution)/shard_map/ppermute | solution.py:18
  204.4 46.1 %collective-permute-start.14 = (f32[4,1,64,128]{3,2,1,0:T(8,128)S(1)}, f32[4,1,64,128]{3,2,1,0:T(8,128)S(1)}, u32[]{:S(2)}, u32[]{:S(2)}) collective-permute-start(f32[4,1,64,128]{3,2,1,0:T(8,128)S(1)} %get-tuple-element.14), channel_id=1, source_target_pairs={{0,8},{8,16},{16,24},{24,32},{32,40},{40,48},{48,56},{1,9},{9,17},... | collective-permute-start | bytes 393224 | tf_op jit(solution)/shard_map/ppermute | solution.py:17
  206.4 45.5 %collective-permute-start.15 = (f32[4,1,64,128]{3,2,1,0:T(8,128)S(1)}, f32[4,1,64,128]{3,2,1,0:T(8,128)S(1)}, u32[]{:S(2)}, u32[]{:S(2)}) collective-permute-start(f32[4,1,64,128]{3,2,1,0:T(8,128)S(1)} %get-tuple-element.15), channel_id=1, source_target_pairs={{8,0},{16,8},{24,16},{32,24},{40,32},{48,40},{56,48},{9,1},{17,9},... | collective-permute-start | bytes 393224 | tf_op jit(solution)/shard_map/ppermute | solution.py:18
  212.9 39.1 %collective-permute-start.16 = (f32[4,64,1,128]{3,1,2,0:T(8,128)S(1)}, f32[4,64,1,128]{3,1,2,0:T(8,128)S(1)}, u32[]{:S(2)}, u32[]{:S(2)}) collective-permute-start(f32[4,64,1,128]{3,1,2,0:T(8,128)S(1)} %bitcast.38), channel_id=1, source_target_pairs={{0,1},{1,2},{2,3},{3,4},{4,5},{5,6},{6,7},{8,9},{9,10},{10,11},{11... | collective-permute-start | bytes 393224 | tf_op jit(solution)/shard_map/ppermute | solution.py:17
  250.4 5.4 %collective-permute-start.17 = (f32[4,64,1,128]{3,1,2,0:T(8,128)S(1)}, f32[4,64,1,128]{3,1,2,0:T(8,128)S(1)}, u32[]{:S(2)}, u32[]{:S(2)}) collective-permute-start(f32[4,64,1,128]{3,1,2,0:T(8,128)S(1)} %bitcast.35), channel_id=1, source_target_pairs={{1,0},{2,1},{3,2},{4,3},{5,4},{6,5},{7,6},{9,8},{10,9},{11,10},{12... | collective-permute-start | bytes 393224 | tf_op jit(solution)/shard_map/ppermute | solution.py:18
  286.6 62.3 %collective-permute-start.18 = (f32[1,64,64,128]{3,2,1,0:T(8,128)S(1)}, f32[1,64,64,128]{3,2,1,0:T(8,128)S(1)}, u32[]{:S(2)}, u32[]{:S(2)}) collective-permute-start(f32[1,64,64,128]{3,2,1,0:T(8,128)S(1)} %get-tuple-element.6), channel_id=1, source_target_pairs={{0,64},{1,65},{2,66},{3,67},{4,68},{5,69},{6,70},{7,71},{8,72},{9,... | collective-permute-start | bytes 6291464 | tf_op jit(solution)/shard_map/ppermute | solution.py:17
  287.9 61.0 %collective-permute-start.19 = (f32[1,64,64,128]{3,2,1,0:T(8,128)S(1)}, f32[1,64,64,128]{3,2,1,0:T(8,128)}, u32[]{:S(2)}, u32[]{:S(2)}) collective-permute-start(f32[1,64,64,128]{3,2,1,0:T(8,128)S(1)} %get-tuple-element.7), channel_id=1, source_target_pairs={{64,0},{65,1},{66,2},{67,3},{68,4},{69,5},{70,6},{71,7},{72,8},{73... | collective-permute-start | bytes 6291464 | tf_op jit(solution)/shard_map/ppermute | solution.py:18
  296.5 46.1 %collective-permute-start.20 = (f32[4,1,64,128]{3,2,1,0:T(8,128)S(1)}, f32[4,1,64,128]{3,2,1,0:T(8,128)S(1)}, u32[]{:S(2)}, u32[]{:S(2)}) collective-permute-start(f32[4,1,64,128]{3,2,1,0:T(8,128)S(1)} %get-tuple-element.8), channel_id=1, source_target_pairs={{0,8},{8,16},{16,24},{24,32},{32,40},{40,48},{48,56},{1,9},{9,17},... | collective-permute-start | bytes 393224 | tf_op jit(solution)/shard_map/ppermute | solution.py:17
  299.8 48.2 %collective-permute-start.21 = (f32[4,1,64,128]{3,2,1,0:T(8,128)S(1)}, f32[4,1,64,128]{3,2,1,0:T(8,128)S(1)}, u32[]{:S(2)}, u32[]{:S(2)}) collective-permute-start(f32[4,1,64,128]{3,2,1,0:T(8,128)S(1)} %get-tuple-element.9), channel_id=1, source_target_pairs={{8,0},{16,8},{24,16},{32,24},{40,32},{48,40},{56,48},{9,1},{17,9},... | collective-permute-start | bytes 393224 | tf_op jit(solution)/shard_map/ppermute | solution.py:18
  305.0 43.1 %collective-permute-start.23 = (f32[4,64,1,128]{3,1,2,0:T(8,128)S(1)}, f32[4,64,1,128]{3,1,2,0:T(8,128)S(1)}, u32[]{:S(2)}, u32[]{:S(2)}) collective-permute-start(f32[4,64,1,128]{3,1,2,0:T(8,128)S(1)} %bitcast.36), channel_id=1, source_target_pairs={{1,0},{2,1},{3,2},{4,3},{5,4},{6,5},{7,6},{9,8},{10,9},{11,10},{12... | collective-permute-start | bytes 393224 | tf_op jit(solution)/shard_map/ppermute | solution.py:18
  342.5 6.4 %collective-permute-start.22 = (f32[4,64,1,128]{3,1,2,0:T(8,128)S(1)}, f32[4,64,1,128]{3,1,2,0:T(8,128)S(1)}, u32[]{:S(2)}, u32[]{:S(2)}) collective-permute-start(f32[4,64,1,128]{3,1,2,0:T(8,128)S(1)} %bitcast.33), channel_id=1, source_target_pairs={{0,1},{1,2},{2,3},{3,4},{4,5},{5,6},{6,7},{8,9},{9,10},{10,11},{11... | collective-permute-start | bytes 393224 | tf_op jit(solution)/shard_map/ppermute | solution.py:17
  390.3 49.9 %all-to-all-start = ((f32[2,1,64,64,128]{4,3,2,1,0:T(8,128)}), f32[2,1,64,64,128]{4,3,2,1,0:T(8,128)}, u32[]{:S(2)}, u32[]{:S(2)}) async-start(f32[2,1,64,64,128]{4,3,2,1,0:T(8,128)} %broadcast_in_dim.23), calls=%async_computation | async-start | bytes 8388608 | tf_op jit(solution)/shard_map/all_to_all | solution.py:31
  (5 other events, 33.0 us)
where the time goes:
time: 461 us; the launch traced here: 452 us
  waiting for transfers between devices  202 us (44%)
  other arithmetic  131 us (28%)
  starting transfers between devices  84.4 us (18%)
  local copies, waits for them, and re-layouts  33.6 us (7%)
    ppermute x12, waiting for transfers between devices, extended(): lax.ppermute(last, axis, up)  152 us
    add x4, other arithmetic, one_step(): return middle + mobility * spread + source  111 us
    ppermute x12, starting transfers between devices, extended(): lax.ppermute(first, axis, [(b, a) for a, b in up])  49.8 us
    all_to_all x1, waiting for transfers between devices, sent_to_all(): lax.all_to_all(jnp.broadcast_to(array[None], (count, *array.shape)), axis...  44.3 us
    ppermute x12, starting transfers between devices, extended(): lax.ppermute(last, axis, up)  29.1 us
    slice x11, local copies, waits for them, and re-layouts, extended(): last = lax.slice_in_dim(array, length - width, length, axis=dim)  16 us
  transfers between devices with their start and end apart: 25, of which 9 were waited for; matrix products, arithmetic and copies ran while one was open for 4% of the time, Pallas kernels for 0%

commit v1 on v0

v1 whole, which is shorter than its diff:
```python
import functools

import jax
import jax.numpy as jnp
from jax import lax
from jax.experimental import pallas as pl
from jax.experimental.pallas import tpu as pltpu
from jax.sharding import PartitionSpec as P

STEPS = 4
CHUNKS = 8
MESH = pl.DeviceIdType.MESH


def kernel(dims, sizes, f_hbm, m_hbm, s_hbm, cs_hbm, fe_hbm, F, M, S, R, T, KS, KR,
           ld_sem, e_send, e_recv, h_send, h_recv, k_send, k_recv, out_sem):
    J, I, K, L = dims
    n_rows, n_cols, n_slabs = sizes
    W = I // CHUNKS
    r = lax.axis_index("rows")
    c = lax.axis_index("cols")
    s = lax.axis_index("slabs")
    other = 1 - r
    edge = (J - 1) * (1 - r)
    edge_in = (J - 2) * (1 - r) + r
    far = (J - 1) * r
    far_in = (1 - r) + (J - 2) * r
    has_low, has_high = c > 0, c < n_cols - 1
    has_front, has_back = s > 0, s < n_slabs - 1

    def rows_of(chunk, extra=0):
        return pl.ds(chunk * W + extra, W)

    def e_copy(t, chunk):
        if t == 0:
            src = f_hbm.at[edge, rows_of(chunk)]
        elif t < STEPS:
            src = F.at[t % 2, edge, rows_of(chunk, 1)]
        else:
            src = T.at[rows_of(chunk)]
        return pltpu.make_async_remote_copy(
            src_ref=src, dst_ref=R.at[t, rows_of(chunk)],
            send_sem=e_send.at[t, chunk], recv_sem=e_recv.at[t, chunk],
            device_id={"rows": other}, device_id_type=MESH)

    def h_copy(t, up):
        row = I - 1 if up else 0
        src = f_hbm.at[:, row] if t == 0 else F.at[t % 2, :, row + 1]
        return pltpu.make_async_remote_copy(
            src_ref=src, dst_ref=F.at[t % 2, :, 0 if up else I + 1],
            send_sem=h_send.at[t, up], recv_sem=h_recv.at[t, up],
            device_id={"cols": c + 1 if up else c - 1}, device_id_type=MESH)

    def k_copy(t, up, chunk):
        return pltpu.make_async_remote_copy(
            src_ref=KS.at[t, up, :, rows_of(chunk)], dst_ref=KR.at[t, up, :, rows_of(chunk)],
            send_sem=k_send.at[t, up, chunk], recv_sem=k_recv.at[t, up, chunk],
            device_id={"slabs": s + 1 if up else s - 1}, device_id_type=MESH)

    def load(which, chunk):
        hbm = (f_hbm, m_hbm, s_hbm)[which]
        dst = (F.at[0, :, rows_of(chunk, 1)], M.at[:, rows_of(chunk)], S.at[:, rows_of(chunk)])[which]
        return pltpu.make_async_copy(hbm.at[:, rows_of(chunk)], dst, ld_sem.at[which, chunk])

    def put(which, chunk):
        src = (M.at[:, rows_of(chunk)], F.at[STEPS % 2, :, rows_of(chunk, 1)])[which]
        dst = (cs_hbm, fe_hbm)[which]
        return pltpu.make_async_copy(src, dst.at[:, rows_of(chunk)], out_sem.at[which, chunk])

    def loop(n, body):
        def step(i, carry):
            body(i)
            return carry
        lax.fori_loop(0, n, step, 0)

    def chunk_at(pos):
        return (pos + CHUNKS - 1) % CHUNKS

    barrier = pltpu.get_barrier_semaphore()
    greet = [(None, {"rows": other}), (has_low, {"cols": c - 1}), (has_high, {"cols": c + 1}),
             (has_front, {"slabs": s - 1}), (has_back, {"slabs": s + 1})]
    for cond, target in greet:
        def signal(target=target):
            pl.semaphore_signal(barrier, inc=1, device_id=target, device_id_type=MESH)
        signal() if cond is None else pl.when(cond)(signal)
    loop(CHUNKS, lambda i: load(0, i).start())
    peers = (1 + (c + n_cols - 1) // n_cols + (2 * n_cols - 2 - c) // n_cols
             + (s + n_slabs - 1) // n_slabs + (2 * n_slabs - 2 - s) // n_slabs)
    pl.semaphore_wait(barrier, peers)

    pl.when(has_high)(lambda: h_copy(0, 1).start())
    e_copy(0, CHUNKS - 1).start()
    pl.when(has_low)(lambda: h_copy(0, 0).start())
    loop(CHUNKS - 1, lambda i: e_copy(0, i).start())
    for which in (1, 2):
        loop(CHUNKS, lambda i: load(which, i).start())

    zero_row = jnp.zeros((K, L), jnp.float32)
    for cond, row in ((c == 0, 0), (c == n_cols - 1, I + 1)):
        @pl.when(cond)
        def _():
            for slot in range(2):
                for p in range(J):
                    F[slot, p, row] = zero_row
    for cond, up in ((s == 0, 1), (s == n_slabs - 1, 0)):
        @pl.when(cond)
        def _():
            def clear(t):
                for p in range(J):
                    KR[t, up, p] = jnp.zeros((I, L), jnp.float32)
            loop(STEPS, clear)

    def send_faces(t, chunk):
        pl.when(has_front)(lambda: k_copy(t, 0, chunk).start())
        pl.when(has_back)(lambda: k_copy(t, 1, chunk).start())

    loop(CHUNKS, lambda i: load(0, i).wait())

    def first_faces(pos):
        chunk = chunk_at(pos)
        for p in range(J):
            def one(i, p=p):
                row = chunk * W + i
                x = F[0, p, row + 1]
                KS[0, 0, p, pl.ds(row, 1), :] = x[0:1]
                KS[0, 1, p, pl.ds(row, 1), :] = x[K - 1:K]
            loop(W, one)
        send_faces(0, chunk)
    loop(CHUNKS, first_faces)

    k_index = lax.broadcasted_iota(jnp.int32, (K, L), 0)

    def stencil_row(t, p, row, near):
        now, later = t % 2, (t + 1) % 2
        x = F[now, p, row + 1]
        below = jnp.where(k_index == 0, KR[t, 1, p, pl.ds(row, 1), :], pltpu.roll(x, 1, 0))
        above = jnp.where(k_index == K - 1, KR[t, 0, p, pl.ds(row, 1), :], pltpu.roll(x, K - 1, 0))
        total = near(row) + (F[now, p, row] + F[now, p, row + 2]) + (below + above) - 6.0 * x
        y = x + M[p, row] * total + S[p, row]
        F[later, p, row + 1] = y
        if t < STEPS - 1:
            KS[t + 1, 0, p, pl.ds(row, 1), :] = y[0:1]
            KS[t + 1, 1, p, pl.ds(row, 1), :] = y[K - 1:K]

    def step_chunk(t, chunk):
        now = t % 2
        if t == 0:
            load(1, chunk).wait()
            load(2, chunk).wait()
        first, last = chunk == 0, chunk == CHUNKS - 1
        pl.when(has_front)(lambda: k_copy(t, 1, chunk).wait_recv())
        pl.when(has_back)(lambda: k_copy(t, 0, chunk).wait_recv())
        pl.when(first & has_low)(lambda: h_copy(t, 1).wait_recv())
        pl.when(last & has_high)(lambda: h_copy(t, 0).wait_recv())
        if t > 0:
            pl.when(first & has_low)(lambda: h_copy(t - 1, 0).wait_send())
            pl.when(last & has_high)(lambda: h_copy(t - 1, 1).wait_send())
            e_copy(t - 1, chunk).wait_send()
        e_copy(t, chunk).wait_recv()
        base = chunk * W
        loop(W, lambda i: stencil_row(
            t, edge, base + i, lambda row: F[now, edge_in, row + 1] + R[t, row]))
        if t < STEPS - 1:
            e_copy(t + 1, chunk).start()
        loop(W, lambda i: stencil_row(
            t, far, base + i, lambda row: F[now, far_in, row + 1]))
        for p in range(1, J - 1):
            loop(W, lambda i, p=p: stencil_row(
                t, p, base + i, lambda row: F[now, p - 1, row + 1] + F[now, p + 1, row + 1]))
        if t < STEPS - 1:
            pl.when(first & has_low)(lambda: h_copy(t + 1, 0).start())
            pl.when(last & has_high)(lambda: h_copy(t + 1, 1).start())
            send_faces(t + 1, chunk)
        else:
            put(1, chunk).start()

            @pl.when(r == 0)
            def _():
                def totals(i):
                    row = base + i
                    total = F[STEPS % 2, 0, row + 1]
                    M[0, row] = total * (1.0 / (J * n_rows))
                    for p in range(1, J):
                        total = total + F[STEPS % 2, p, row + 1]
                        M[p, row] = total * (1.0 / (J * n_rows))
                    T[row] = total
                loop(W, totals)
                e_copy(STEPS, chunk).start()
                put(0, chunk).start()

    for t in range(STEPS):
        loop(CHUNKS, lambda pos, t=t: step_chunk(t, chunk_at(pos)))

    @pl.when(r == 1)
    def _():
        def finish(pos):
            chunk = chunk_at(pos)
            e_copy(STEPS, chunk).wait_recv()

            def sums(i):
                row = chunk * W + i
                total = R[STEPS, row]
                for p in range(J):
                    total = total + F[STEPS % 2, p, row + 1]
                    M[p, row] = total * (1.0 / (J * n_rows))
            loop(W, sums)
            put(0, chunk).start()
        loop(CHUNKS, finish)

    pl.when(has_low)(lambda: h_copy(STEPS - 1, 0).wait_send())
    pl.when(has_high)(lambda: h_copy(STEPS - 1, 1).wait_send())

    def drain(i):
        e_copy(STEPS - 1, i).wait_send()
        pl.when(r == 0)(lambda: e_copy(STEPS, i).wait_send())
        for t in range(STEPS):
            pl.when(has_front)(lambda t=t: k_copy(t, 0, i).wait_send())
            pl.when(has_back)(lambda t=t: k_copy(t, 1, i).wait_send())
        put(0, i).wait()
        put(1, i).wait()
    loop(CHUNKS, drain)


def local(sizes, field_values, mobility, source):
    J, I, K, L = field_values.shape
    f32 = jnp.float32
    any_space = pl.BlockSpec(memory_space=pl.ANY)
    dma = pltpu.SemaphoreType.DMA
    return tuple(pl.pallas_call(
        functools.partial(kernel, (J, I, K, L), sizes),
        out_shape=[jax.ShapeDtypeStruct((J, I, K, L), f32)] * 2,
        in_specs=[any_space] * 3,
        out_specs=[any_space] * 2,
        scratch_shapes=[
            pltpu.VMEM((2, J, I + 2, K, L), f32),
            pltpu.VMEM((J, I, K, L), f32),
            pltpu.VMEM((J, I, K, L), f32),
            pltpu.VMEM((STEPS + 1, I, K, L), f32),
            pltpu.VMEM((I, K, L), f32),
            pltpu.VMEM((STEPS, 2, J, I, L), f32),
            pltpu.VMEM((STEPS, 2, J, I, L), f32),
            dma((3, CHUNKS)),
            dma((STEPS + 1, CHUNKS)),
            dma((STEPS + 1, CHUNKS)),
            dma((STEPS, 2)),
            dma((STEPS, 2)),
            dma((STEPS, 2, CHUNKS)),
            dma((STEPS, 2, CHUNKS)),
            dma((2, CHUNKS)),
        ],
        compiler_params=pltpu.CompilerParams(
            collective_id=0, has_side_effects=True, vmem_limit_bytes=60 * 1024 * 1024),
        name="diffuse",
    )(field_values, mobility, source))


def solution(mesh):
    spec = P("rows", "cols", "slabs", None)
    sizes = tuple(mesh.shape[axis] for axis in ("rows", "cols", "slabs"))
    return jax.shard_map(functools.partial(local, sizes), mesh=mesh,
                         in_specs=(spec,) * 3, out_specs=(spec,) * 2, check_vma=False)
```

time: 461 us -> 268 us (0.58); the launches traced: 452 us -> 267 us
  Pallas kernels: 0 us -> 255 us
  waiting for transfers between devices: 202 us -> 0 us
  other arithmetic: 131 us -> 0 us
  starting transfers between devices: 84.4 us -> 0 us
  local copies, waits for them, and re-layouts: 33.6 us -> 12 us
    pallas_call x0 -> x1, Pallas kernels: none -> 255 us  [local(): pl.pallas_call(functools.partial(kernel, (J, I, K, L), sizes), out_shape=...]
    ppermute x24 -> x0, waiting for transfers between devices: 157 us -> none  [the longest x12 152 us: extended(): lax.ppermute(last, axis, up)]
    add x5 -> x0, other arithmetic: 111 us -> none  [the longest x4 111 us: one_step(): return middle + mobility * spread + source]
    ppermute x24 -> x0, starting transfers between devices: 78.9 us -> none  [the longest x12 49.8 us: extended(): lax.ppermute(first, axis, [(b, a) for a, b in up])]
    all_to_all x1 -> x0, waiting for transfers between devices: 44.3 us -> none  [sent_to_all(): lax.all_to_all(jnp.broadcast_to(array[None], (count, *array.shape)), axis...]
    slice x12 -> x0, local copies, waits for them, and re-layouts: 20.1 us -> none  [the longest x11 16 us: extended(): last = lax.slice_in_dim(array, length - width, length, axis=dim)]
    div x1 -> x0, other arithmetic: 8.78 us -> none  [local(): (here + below) / (field_values.shape[0] * lax.axis_size('rows'))]
    another operation x1 -> x0, other arithmetic: 8.69 us -> none  [local(): here = jnp.cumsum(field_values, axis=0)]
  transfers between devices with their start and end apart: 25 -> 0, of which waited for: 9 -> 0; matrix products, arithmetic and copies ran while one was open for 4% -> 0% of each run, Pallas kernels for 0% -> 0%
where the time goes in v1:
time: 268 us; the launch traced here: 267 us
  Pallas kernels  255 us (95%)
  local copies, waits for them, and re-layouts  12 us (4%)
    pallas_call x1, Pallas kernels, local(): pl.pallas_call(functools.partial(kernel, (J, I, K, L), sizes), out_shape=...  255 us
    unnamed x4, local copies, waits for them, and re-layouts  12 us

profile of v1, /device:TPU:112, one launch (start us, length us, event | category | flops | bytes accessed | tf_op | source)
XLA Modules:
  0.0 267.5 jit_solution(9091063969063811132)
XLA Ops:
  0.6 254.8 %diffuse.1 = (f32[4,64,64,128]{3,2,1,0:T(8,128)}, f32[4,64,64,128]{3,2,1,0:T(8,128)}) custom-call(f32[4,64,64,128]{3,2,1,0:T(8,128)} %f_hbm.1, f32[4,64,64,128]{3,2,1,0:T(8,128)} %m_hbm.1, f32[4,64,64,128]{3,2,1,0:T(8,128)} %s_hbm.1), custom_call_target="tpu_custom_call" | custom-call | tf_op jit(solution)/shard_map/diffuse/pallas_call | solution.py:229
  255.5 0.0 copy-start
  255.5 8.6 %copy.7 = f32[4,64,64,128]{3,2,1,0:T(8,128)} copy(f32[4,64,64,128]{3,2,1,0:T(8,128)} %get-tuple-element.4) | data formatting | bytes 16777216
  264.1 0.0 copy-done
  264.1 3.4 %copy.8 = f32[4,64,64,128]{3,2,1,0:T(8,128)} copy(f32[4,64,64,128]{3,2,1,0:T(8,128)S(1)} %copy-done) | data formatting | bytes 16777216
Async XLA Ops:
  255.5 8.6 %copy-start = (f32[4,64,64,128]{3,2,1,0:T(8,128)S(1)}, f32[4,64,64,128]{3,2,1,0:T(8,128)}, u32[]{:S(2)}) copy-start(f32[4,64,64,128]{3,2,1,0:T(8,128)} %get-tuple-element.5) | copy-start | bytes 25165828

commit v2 on v1

v2 whole, which is shorter than its diff:
```python
import functools

import jax
import jax.numpy as jnp
from jax import lax
from jax.experimental import pallas as pl
from jax.experimental.pallas import tpu as pltpu
from jax.sharding import PartitionSpec as P

STEPS = 4
CHUNKS = 16
FIRST = 6
AHEAD = 8
MESH = pl.DeviceIdType.MESH


def kernel(dims, sizes, f_hbm, m_hbm, s_hbm, M, S, F, R, T, KS, KR,
           ld_sem, e_send, e_recv, h_send, h_recv, k_send, k_recv):
    J, I, K, L = dims
    n_rows, n_cols, n_slabs = sizes
    W = I // CHUNKS
    r = lax.axis_index("rows")
    c = lax.axis_index("cols")
    s = lax.axis_index("slabs")
    other = 1 - r
    edge = (J - 1) * (1 - r)
    edge_in = (J - 2) * (1 - r) + r
    far = (J - 1) * r
    far_in = (1 - r) + (J - 2) * r
    has_low, has_high = c > 0, c < n_cols - 1
    has_front, has_back = s > 0, s < n_slabs - 1

    def rows_of(chunk, extra=0):
        return pl.ds(chunk * W + extra, W)

    def chunk_at(pos):
        return (pos + FIRST) % CHUNKS

    def edge_rows(t, chunk):
        if t == 0:
            return f_hbm.at[edge, rows_of(chunk)]
        if t < STEPS:
            return F.at[t % 2, edge, rows_of(chunk, 1)]
        return T.at[rows_of(chunk)]

    def e_copy(t, pos):
        chunk = chunk_at(pos)
        return pltpu.make_async_remote_copy(
            src_ref=edge_rows(t, chunk), dst_ref=R.at[t % 2, rows_of(chunk)],
            send_sem=e_send.at[t % 2, pos], recv_sem=e_recv.at[t % 2, pos],
            device_id={"rows": other}, device_id_type=MESH)

    def h_copy(t, up):
        row = I - 1 if up else 0
        src = f_hbm.at[:, row] if t == 0 else F.at[t % 2, :, row + 1]
        return pltpu.make_async_remote_copy(
            src_ref=src, dst_ref=F.at[t % 2, :, 0 if up else I + 1],
            send_sem=h_send.at[t, up], recv_sem=h_recv.at[t, up],
            device_id={"cols": c + 1 if up else c - 1}, device_id_type=MESH)

    def k_copy(t, up, pos):
        chunk = chunk_at(pos)
        return pltpu.make_async_remote_copy(
            src_ref=KS.at[t % 2, up, :, rows_of(chunk)], dst_ref=KR.at[t % 2, up, :, rows_of(chunk)],
            send_sem=k_send.at[t % 2, up, pos], recv_sem=k_recv.at[t % 2, up, pos],
            device_id={"slabs": s + 1 if up else s - 1}, device_id_type=MESH)

    def load(which, pos):
        chunk = chunk_at(pos)
        hbm = (f_hbm, m_hbm, s_hbm)[which]
        dst = (F.at[0, :, rows_of(chunk, 1)], M.at[:, rows_of(chunk)], S.at[:, rows_of(chunk)])[which]
        return pltpu.make_async_copy(hbm.at[:, rows_of(chunk)], dst, ld_sem.at[which, pos])

    def loop(n, body):
        def step(i, carry):
            body(i)
            return carry
        lax.fori_loop(0, n, step, 0)

    def send(t, pos):
        e_copy(t, pos).start()

    barrier = pltpu.get_barrier_semaphore()
    greet = [(None, {"rows": other}), (has_low, {"cols": c - 1}), (has_high, {"cols": c + 1}),
             (has_front, {"slabs": s - 1}), (has_back, {"slabs": s + 1})]
    for cond, target in greet:
        def signal(target=target):
            pl.semaphore_signal(barrier, inc=1, device_id=target, device_id_type=MESH)
        signal() if cond is None else pl.when(cond)(signal)
    loop(CHUNKS, lambda i: load(0, i).start())
    peers = (1 + (c + n_cols - 1) // n_cols + (2 * n_cols - 2 - c) // n_cols
             + (s + n_slabs - 1) // n_slabs + (2 * n_slabs - 2 - s) // n_slabs)
    pl.semaphore_wait(barrier, peers)

    loop(AHEAD, lambda i: send(0, i))

    pl.when(has_high)(lambda: h_copy(0, 1).start())
    pl.when(has_low)(lambda: h_copy(0, 0).start())
    for which in (1, 2):
        loop(CHUNKS, lambda i: load(which, i).start())

    zero_row = jnp.zeros((K, L), jnp.float32)
    for cond, row in ((c == 0, 0), (c == n_cols - 1, I + 1)):
        @pl.when(cond)
        def _():
            for slot in range(2):
                for p in range(J):
                    F[slot, p, row] = zero_row
    for cond, up in ((s == 0, 1), (s == n_slabs - 1, 0)):
        @pl.when(cond)
        def _():
            for slot in range(2):
                for p in range(J):
                    KR[slot, up, p] = jnp.zeros((I, L), jnp.float32)

    def send_faces(t, pos):
        pl.when(has_front)(lambda: k_copy(t, 0, pos).start())
        pl.when(has_back)(lambda: k_copy(t, 1, pos).start())

    loop(CHUNKS, lambda i: load(0, i).wait())

    def first_faces(pos):
        chunk = chunk_at(pos)
        for p in range(J):
            def one(i, p=p):
                row = chunk * W + i
                x = F[0, p, row + 1]
                KS[0, 0, p, pl.ds(row, 1), :] = x[0:1]
                KS[0, 1, p, pl.ds(row, 1), :] = x[K - 1:K]
            loop(W, one)
        send_faces(0, pos)
    loop(CHUNKS, first_faces)

    k_index = lax.broadcasted_iota(jnp.int32, (K, L), 0)

    def stencil_row(t, p, row, near):
        now, later = t % 2, (t + 1) % 2
        x = F[now, p, row + 1]
        below = jnp.where(k_index == 0, KR[now, 1, p, pl.ds(row, 1), :], pltpu.roll(x, 1, 0))
        above = jnp.where(k_index == K - 1, KR[now, 0, p, pl.ds(row, 1), :], pltpu.roll(x, K - 1, 0))
        total = near(row) + (F[now, p, row] + F[now, p, row + 2]) + (below + above) - 6.0 * x
        y = x + M[p, row] * total + S[p, row]
        if t == STEPS - 1:
            S[p, row] = y
        else:
            F[later, p, row + 1] = y
        if t < STEPS - 1:
            KS[later, 0, p, pl.ds(row, 1), :] = y[0:1]
            KS[later, 1, p, pl.ds(row, 1), :] = y[K - 1:K]

    def step_chunk(t, pos):
        now = t % 2
        chunk = chunk_at(pos)
        if t == 0:
            load(1, pos).wait()
            load(2, pos).wait()
        first, last = chunk == 0, chunk == CHUNKS - 1
        e_copy(t, pos).wait_recv()
        pl.when(pos < CHUNKS - AHEAD)(lambda: send(t, pos + AHEAD))
        late = pos >= CHUNKS - AHEAD
        if t == STEPS - 1:
            late = late & (r == 0)
        pl.when(late)(lambda: send(t + 1, pos + AHEAD - CHUNKS))
        pl.when(has_front)(lambda: k_copy(t, 1, pos).wait_recv())
        pl.when(has_back)(lambda: k_copy(t, 0, pos).wait_recv())
        pl.when(first & has_low)(lambda: h_copy(t, 1).wait_recv())
        pl.when(last & has_high)(lambda: h_copy(t, 0).wait_recv())
        if t > 0:
            pl.when(first & has_low)(lambda: h_copy(t - 1, 0).wait_send())
            pl.when(last & has_high)(lambda: h_copy(t - 1, 1).wait_send())
            pl.when(has_front)(lambda: k_copy(t - 1, 0, pos).wait_send())
            pl.when(has_back)(lambda: k_copy(t - 1, 1, pos).wait_send())
            e_copy(t - 1, pos).wait_send()
        base = chunk * W
        loop(W, lambda i: stencil_row(
            t, edge, base + i, lambda row: F[now, edge_in, row + 1] + R[now, row]))
        loop(W, lambda i: stencil_row(
            t, far, base + i, lambda row: F[now, far_in, row + 1]))
        for p in range(1, J - 1):
            loop(W, lambda i, p=p: stencil_row(
                t, p, base + i, lambda row: F[now, p - 1, row + 1] + F[now, p + 1, row + 1]))
        if t < STEPS - 1:
            pl.when(first & has_low)(lambda: h_copy(t + 1, 0).start())
            pl.when(last & has_high)(lambda: h_copy(t + 1, 1).start())
            send_faces(t + 1, pos)
        else:
            @pl.when(r == 0)
            def _():
                def totals(i):
                    row = base + i
                    total = S[0, row]
                    M[0, row] = total * (1.0 / (J * n_rows))
                    for p in range(1, J):
                        total = total + S[p, row]
                        M[p, row] = total * (1.0 / (J * n_rows))
                    T[row] = total
                loop(W, totals)

    for t in range(STEPS):
        loop(CHUNKS, lambda pos, t=t: step_chunk(t, pos))

    @pl.when(r == 0)
    def _():
        loop(CHUNKS - AHEAD, lambda i: send(STEPS, i + AHEAD))

    @pl.when(r == 1)
    def _():
        def finish(pos):
            e_copy(STEPS, pos).wait_recv()

            def sums(i):
                row = chunk_at(pos) * W + i
                total = R[STEPS % 2, row]
                for p in range(J):
                    total = total + S[p, row]
                    M[p, row] = total * (1.0 / (J * n_rows))
            loop(W, sums)
        loop(CHUNKS, finish)

    pl.when(has_low)(lambda: h_copy(STEPS - 1, 0).wait_send())
    pl.when(has_high)(lambda: h_copy(STEPS - 1, 1).wait_send())

    def drain(i):
        e_copy(STEPS - 1, i).wait_send()
        pl.when(r == 0)(lambda: e_copy(STEPS, i).wait_send())
        pl.when(has_front)(lambda: k_copy(STEPS - 1, 0, i).wait_send())
        pl.when(has_back)(lambda: k_copy(STEPS - 1, 1, i).wait_send())
    loop(CHUNKS, drain)


def write_out(cs_vmem, fe_vmem, cs_hbm, fe_hbm, sem):
    W = cs_vmem.shape[1] // CHUNKS

    def put(which, i):
        src, dst = ((cs_vmem, cs_hbm), (fe_vmem, fe_hbm))[which]
        rows = pl.ds(i * W, W)
        return pltpu.make_async_copy(src.at[:, rows], dst.at[:, rows], sem.at[which, i])

    for i in range(CHUNKS):
        put(0, i).start()
        put(1, i).start()
    for i in range(CHUNKS):
        put(0, i).wait()
        put(1, i).wait()


def local(sizes, field_values, mobility, source):
    J, I, K, L = field_values.shape
    f32 = jnp.float32
    vmem = pl.BlockSpec(memory_space=pltpu.VMEM)
    any_space = pl.BlockSpec(memory_space=pl.ANY)
    dma = pltpu.SemaphoreType.DMA
    column_sum, field_end = pl.pallas_call(
        functools.partial(kernel, (J, I, K, L), sizes),
        out_shape=[pltpu.VMEM((J, I, K, L), f32)] * 2,
        in_specs=[any_space] * 3,
        out_specs=[vmem] * 2,
        scratch_shapes=[
            pltpu.VMEM((2, J, I + 2, K, L), f32),
            pltpu.VMEM((2, I, K, L), f32),
            pltpu.VMEM((I, K, L), f32),
            pltpu.VMEM((2, 2, J, I, L), f32),
            pltpu.VMEM((2, 2, J, I, L), f32),
            dma((3, CHUNKS)),
            dma((2, CHUNKS)),
            dma((2, CHUNKS)),
            dma((STEPS, 2)),
            dma((STEPS, 2)),
            dma((2, 2, CHUNKS)),
            dma((2, 2, CHUNKS)),
        ],
        compiler_params=pltpu.CompilerParams(
            collective_id=0, has_side_effects=True, vmem_limit_bytes=32 * 1024 * 1024),
        name="diffuse",
    )(field_values, mobility, source)
    return tuple(pl.pallas_call(
        write_out,
        out_shape=[jax.ShapeDtypeStruct((J, I, K, L), f32)] * 2,
        in_specs=[vmem] * 2,
        out_specs=[any_space] * 2,
        scratch_shapes=[dma((2, CHUNKS))],
        compiler_params=pltpu.CompilerParams(vmem_limit_bytes=1024 * 1024),
        name="write_out",
    )(column_sum, field_end))


def solution(mesh):
    spec = P("rows", "cols", "slabs", None)
    sizes = tuple(mesh.shape[axis] for axis in ("rows", "cols", "slabs"))
    return jax.shard_map(functools.partial(local, sizes), mesh=mesh,
                         in_specs=(spec,) * 3, out_specs=(spec,) * 2, check_vma=False)
```

time: 268 us -> 261 us (0.974)
  local copies, waits for them, and re-layouts: 12 us -> 0 us
  Pallas kernels: 255 us -> 260 us
    unnamed x4 -> x0, local copies, waits for them, and re-layouts: 12 us -> none
    pallas_call x0 -> x1, Pallas kernels: none -> 6.08 us  [local(): pl.pallas_call(write_out, out_shape=[jax.ShapeDtypeStruct((J, I, K, L), f...]
where the time goes in v2:
time: 261 us
  Pallas kernels  260 us (100%)
    pallas_call x1, Pallas kernels, local(): pl.pallas_call(functools.partial(kernel, (J, I, K, L), sizes), out_shape=...  254 us
    pallas_call x1, Pallas kernels, local(): pl.pallas_call(write_out, out_shape=[jax.ShapeDtypeStruct((J, I, K, L), f...  6.08 us

profile of v2, /device:TPU:112, one launch (start us, length us, event | category | flops | bytes accessed | tf_op | source)
XLA Modules:
  0.0 260.6 jit_solution(15759228844111546327)
XLA Ops:
  0.6 253.9 %diffuse.1 = (f32[4,64,64,128]{3,2,1,0:T(8,128)S(1)}, f32[4,64,64,128]{3,2,1,0:T(8,128)S(1)}) custom-call(f32[4,64,64,128]{3,2,1,0:T(8,128)} %f_hbm.1, f32[4,64,64,128]{3,2,1,0:T(8,128)} %m_hbm.1, f32[4,64,64,128]{3,2,1,0:T(8,128)} %s_hbm.1), custom_call_target="tpu_custom_call" | custom-call | tf_op jit(solution)/shard_map/diffuse/pallas_call | solution.py:253
  254.6 6.1 %write_out.1 = (f32[4,64,64,128]{3,2,1,0:T(8,128)}, f32[4,64,64,128]{3,2,1,0:T(8,128)}) custom-call(f32[4,64,64,128]{3,2,1,0:T(8,128)S(1)} %get-tuple-element.4.cs_vmem, f32[4,64,64,128]{3,2,1,0:T(8,128)S(1)} %get-tuple-element.5.fe_vmem), custom_call_target="tpu_custom_call" | custom-call | tf_op jit(solution)/shard_map/write_out/pallas_call | solution.py:276

commit v3 on v2

--- a/solution.py
+++ b/solution.py
@@ -10,12 +10,12 @@
 STEPS = 4
 CHUNKS = 16
 FIRST = 6
-AHEAD = 8
+RELAYED = 6
 MESH = pl.DeviceIdType.MESH
 
 
-def kernel(dims, sizes, f_hbm, m_hbm, s_hbm, M, S, F, R, T, KS, KR,
-           ld_sem, e_send, e_recv, h_send, h_recv, k_send, k_recv):
+def kernel(dims, sizes, f_hbm, m_hbm, s_hbm, M, S, F, R, T, B, KS, KR,
+           ld_sem, e_send, e_recv, h_send, h_recv, k_send, k_recv, r_send, r_recv, f_send):
     J, I, K, L = dims
     n_rows, n_cols, n_slabs = sizes
     W = I // CHUNKS
@@ -23,6 +23,7 @@
     c = lax.axis_index("cols")
     s = lax.axis_index("slabs")
     other = 1 - r
+    flip = c + 1 - 2 * (c % 2)
     edge = (J - 1) * (1 - r)
     edge_in = (J - 2) * (1 - r) + r
     far = (J - 1) * r
@@ -33,9 +34,6 @@
     def rows_of(chunk, extra=0):
         return pl.ds(chunk * W + extra, W)
 
-    def chunk_at(pos):
-        return (pos + FIRST) % CHUNKS
-
     def edge_rows(t, chunk):
         if t == 0:
             return f_hbm.at[edge, rows_of(chunk)]
@@ -43,12 +41,23 @@
             return F.at[t % 2, edge, rows_of(chunk, 1)]
         return T.at[rows_of(chunk)]
 
-    def e_copy(t, pos):
-        chunk = chunk_at(pos)
+    def e_copy(t, chunk):
         return pltpu.make_async_remote_copy(
             src_ref=edge_rows(t, chunk), dst_ref=R.at[t % 2, rows_of(chunk)],
-            send_sem=e_send.at[t % 2, pos], recv_sem=e_recv.at[t % 2, pos],
+            send_sem=e_send.at[t % 2, chunk], recv_sem=e_recv.at[t % 2, chunk],
             device_id={"rows": other}, device_id_type=MESH)
+
+    def r_copy(i):
+        return pltpu.make_async_remote_copy(
+            src_ref=T.at[rows_of(FIRST + i)], dst_ref=B.at[i],
+            send_sem=r_send.at[i], recv_sem=r_recv.at[i],
+            device_id={"rows": other, "cols": flip}, device_id_type=MESH)
+
+    def f_copy(i):
+        return pltpu.make_async_remote_copy(
+            src_ref=B.at[i], dst_ref=R.at[STEPS % 2, rows_of(FIRST + i)],
+            send_sem=f_send.at[i], recv_sem=e_recv.at[STEPS % 2, FIRST + i],
+            device_id={"cols": flip}, device_id_type=MESH)
 
     def h_copy(t, up):
         row = I - 1 if up else 0
@@ -58,18 +67,16 @@
             send_sem=h_send.at[t, up], recv_sem=h_recv.at[t, up],
             device_id={"cols": c + 1 if up else c - 1}, device_id_type=MESH)
 
-    def k_copy(t, up, pos):
-        chunk = chunk_at(pos)
+    def k_copy(t, up, chunk):
         return pltpu.make_async_remote_copy(
             src_ref=KS.at[t % 2, up, :, rows_of(chunk)], dst_ref=KR.at[t % 2, up, :, rows_of(chunk)],
-            send_sem=k_send.at[t % 2, up, pos], recv_sem=k_recv.at[t % 2, up, pos],
+            send_sem=k_send.at[t % 2, up, chunk], recv_sem=k_recv.at[t % 2, up, chunk],
             device_id={"slabs": s + 1 if up else s - 1}, device_id_type=MESH)
 
-    def load(which, pos):
-        chunk = chunk_at(pos)
+    def load(which, chunk):
         hbm = (f_hbm, m_hbm, s_hbm)[which]
         dst = (F.at[0, :, rows_of(chunk, 1)], M.at[:, rows_of(chunk)], S.at[:, rows_of(chunk)])[which]
-        return pltpu.make_async_copy(hbm.at[:, rows_of(chunk)], dst, ld_sem.at[which, pos])
+        return pltpu.make_async_copy(hbm.at[:, rows_of(chunk)], dst, ld_sem.at[which, chunk])
 
     def loop(n, body):
         def step(i, carry):
@@ -77,25 +84,27 @@
             return carry
         lax.fori_loop(0, n, step, 0)
 
-    def send(t, pos):
-        e_copy(t, pos).start()
+    def span(start, stop, body):
+        loop(stop - start, lambda i: body(start + i))
 
     barrier = pltpu.get_barrier_semaphore()
-    greet = [(None, {"rows": other}), (has_low, {"cols": c - 1}), (has_high, {"cols": c + 1}),
+    greet = [(None, {"rows": other}), (None, {"rows": other, "cols": flip}),
+             (has_low, {"cols": c - 1}), (has_high, {"cols": c + 1}),
              (has_front, {"slabs": s - 1}), (has_back, {"slabs": s + 1})]
     for cond, target in greet:
         def signal(target=target):
             pl.semaphore_signal(barrier, inc=1, device_id=target, device_id_type=MESH)
         signal() if cond is None else pl.when(cond)(signal)
     loop(CHUNKS, lambda i: load(0, i).start())
-    peers = (1 + (c + n_cols - 1) // n_cols + (2 * n_cols - 2 - c) // n_cols
+    peers = (2 + (c + n_cols - 1) // n_cols + (2 * n_cols - 2 - c) // n_cols
              + (s + n_slabs - 1) // n_slabs + (2 * n_slabs - 2 - s) // n_slabs)
     pl.semaphore_wait(barrier, peers)
 
-    loop(AHEAD, lambda i: send(0, i))
-
     pl.when(has_high)(lambda: h_copy(0, 1).start())
     pl.when(has_low)(lambda: h_copy(0, 0).start())
+    span(FIRST, CHUNKS, lambda i: e_copy(0, i).start())
+    span(0, FIRST, lambda i: e_copy(0, i).start())
+
     for which in (1, 2):
         loop(CHUNKS, lambda i: load(which, i).start())
 
@@ -113,14 +122,13 @@
                 for p in range(J):
                     KR[slot, up, p] = jnp.zeros((I, L), jnp.float32)
 
-    def send_faces(t, pos):
-        pl.when(has_front)(lambda: k_copy(t, 0, pos).start())
-        pl.when(has_back)(lambda: k_copy(t, 1, pos).start())
+    def send_faces(t, chunk):
+        pl.when(has_front)(lambda: k_copy(t, 0, chunk).start())
+        pl.when(has_back)(lambda: k_copy(t, 1, chunk).start())
 
     loop(CHUNKS, lambda i: load(0, i).wait())
 
-    def first_faces(pos):
-        chunk = chunk_at(pos)
+    def first_faces(chunk):
         for p in range(J):
             def one(i, p=p):
                 row = chunk * W + i
@@ -128,8 +136,9 @@
                 KS[0, 0, p, pl.ds(row, 1), :] = x[0:1]
                 KS[0, 1, p, pl.ds(row, 1), :] = x[K - 1:K]
             loop(W, one)
-        send_faces(0, pos)
-    loop(CHUNKS, first_faces)
+        send_faces(0, chunk)
+    span(FIRST, CHUNKS, first_faces)
+    span(0, FIRST, first_faces)
 
     k_index = lax.broadcasted_iota(jnp.int32, (K, L), 0)
 
@@ -148,45 +157,45 @@
             KS[later, 0, p, pl.ds(row, 1), :] = y[0:1]
             KS[later, 1, p, pl.ds(row, 1), :] = y[K - 1:K]
 
-    def step_chunk(t, pos):
+    def send_halo(t, up):
+        pl.when(has_high if up else has_low)(lambda: h_copy(t, up).start())
+
+    def step_chunk(t, chunk, totals=None):
         now = t % 2
-        chunk = chunk_at(pos)
         if t == 0:
-            load(1, pos).wait()
-            load(2, pos).wait()
+            load(1, chunk).wait()
+            load(2, chunk).wait()
         first, last = chunk == 0, chunk == CHUNKS - 1
-        e_copy(t, pos).wait_recv()
-        pl.when(pos < CHUNKS - AHEAD)(lambda: send(t, pos + AHEAD))
-        late = pos >= CHUNKS - AHEAD
-        if t == STEPS - 1:
-            late = late & (r == 0)
-        pl.when(late)(lambda: send(t + 1, pos + AHEAD - CHUNKS))
-        pl.when(has_front)(lambda: k_copy(t, 1, pos).wait_recv())
-        pl.when(has_back)(lambda: k_copy(t, 0, pos).wait_recv())
+        e_copy(t, chunk).wait_recv()
+        pl.when(has_front)(lambda: k_copy(t, 1, chunk).wait_recv())
+        pl.when(has_back)(lambda: k_copy(t, 0, chunk).wait_recv())
         pl.when(first & has_low)(lambda: h_copy(t, 1).wait_recv())
         pl.when(last & has_high)(lambda: h_copy(t, 0).wait_recv())
         if t > 0:
             pl.when(first & has_low)(lambda: h_copy(t - 1, 0).wait_send())
             pl.when(last & has_high)(lambda: h_copy(t - 1, 1).wait_send())
-            pl.when(has_front)(lambda: k_copy(t - 1, 0, pos).wait_send())
-            pl.when(has_back)(lambda: k_copy(t - 1, 1, pos).wait_send())
-            e_copy(t - 1, pos).wait_send()
+            pl.when(has_front)(lambda: k_copy(t - 1, 0, chunk).wait_send())
+            pl.when(has_back)(lambda: k_copy(t - 1, 1, chunk).wait_send())
+            e_copy(t - 1, chunk).wait_send()
         base = chunk * W
         loop(W, lambda i: stencil_row(
             t, edge, base + i, lambda row: F[now, edge_in, row + 1] + R[now, row]))
+        if t < STEPS - 1:
+            e_copy(t + 1, chunk).start()
         loop(W, lambda i: stencil_row(
             t, far, base + i, lambda row: F[now, far_in, row + 1]))
         for p in range(1, J - 1):
             loop(W, lambda i, p=p: stencil_row(
                 t, p, base + i, lambda row: F[now, p - 1, row + 1] + F[now, p + 1, row + 1]))
         if t < STEPS - 1:
-            pl.when(first & has_low)(lambda: h_copy(t + 1, 0).start())
-            pl.when(last & has_high)(lambda: h_copy(t + 1, 1).start())
-            send_faces(t + 1, pos)
+            if t > 0:
+                pl.when(first)(lambda: send_halo(t + 1, 0))
+                pl.when(last)(lambda: send_halo(t + 1, 1))
+            send_faces(t + 1, chunk)
         else:
             @pl.when(r == 0)
             def _():
-                def totals(i):
+                def sums(i):
                     row = base + i
                     total = S[0, row]
                     M[0, row] = total * (1.0 / (J * n_rows))
@@ -194,35 +203,85 @@
                         total = total + S[p, row]
                         M[p, row] = total * (1.0 / (J * n_rows))
                     T[row] = total
-                loop(W, totals)
-
-    for t in range(STEPS):
-        loop(CHUNKS, lambda pos, t=t: step_chunk(t, pos))
+                loop(W, sums)
+                if totals == "relay":
+                    r_copy(chunk - FIRST).start()
+                elif totals == "direct":
+                    e_copy(STEPS, chunk).start()
+
+    def send_totals(*chunks):
+        @pl.when(r == 0)
+        def _():
+            for chunk in chunks:
+                e_copy(STEPS, chunk).start()
+
+    def hand_on(start, stop):
+        @pl.when(r == 1)
+        def _():
+            def one(i):
+                r_copy(i).wait_recv()
+                f_copy(i).start()
+            span(start, stop, one)
+
+    def both_ends(t, a, totals=None):
+        loop(2, lambda i: step_chunk(t, a + i * (CHUNKS - 1 - 2 * a), totals))
+
+    for t in range(STEPS - 1):
+        span(FIRST, CHUNKS - t, lambda chunk: step_chunk(t, chunk))
+        span(t, FIRST, lambda chunk: step_chunk(t, chunk))
+    send_halo(1, 0)
+    send_halo(1, 1)
+    t = STEPS - 1
+    after = FIRST + RELAYED
+    span(FIRST, after, lambda chunk: step_chunk(t, chunk, "relay"))
+    span(after, CHUNKS - t, lambda chunk: step_chunk(t, chunk))
+    span(t, FIRST, lambda chunk: step_chunk(t, chunk))
+    held = list(range(after, CHUNKS - t)) + list(range(t, FIRST))
+    both_ends(1, 0)
+    send_totals(*held[:2])
+    both_ends(2, 1)
+    both_ends(2, 0)
+    send_totals(*held[2:])
+    both_ends(3, 2, "direct")
+    hand_on(0, RELAYED // 2)
+    both_ends(3, 1, "direct")
+    both_ends(3, 0, "direct")
+    hand_on(RELAYED // 2, RELAYED)
 
     @pl.when(r == 0)
     def _():
-        loop(CHUNKS - AHEAD, lambda i: send(STEPS, i + AHEAD))
+        for chunk in range(CHUNKS):
+            if not FIRST <= chunk < after:
+                e_copy(STEPS, chunk).wait_send()
+        for i in range(RELAYED):
+            r_copy(i).wait_send()
 
     @pl.when(r == 1)
     def _():
-        def finish(pos):
-            e_copy(STEPS, pos).wait_recv()
+        def finish(chunk):
+            e_copy(STEPS, chunk).wait_recv()
 
             def sums(i):
-                row = chunk_at(pos) * W + i
+                row = chunk * W + i
                 total = R[STEPS % 2, row]
                 for p in range(J):
                     total = total + S[p, row]
                     M[p, row] = total * (1.0 / (J * n_rows))
             loop(W, sums)
-        loop(CHUNKS, finish)
+        span(after, CHUNKS - t, finish)
+        span(t, FIRST, finish)
+        for a in (2, 1):
+            loop(2, lambda i: finish(a + i * (CHUNKS - 1 - 2 * a)))
+        span(FIRST, after, finish)
+        loop(2, lambda i: finish(i * (CHUNKS - 1)))
+        for i in range(RELAYED):
+            f_copy(i).wait_send()
 
     pl.when(has_low)(lambda: h_copy(STEPS - 1, 0).wait_send())
     pl.when(has_high)(lambda: h_copy(STEPS - 1, 1).wait_send())
 
     def drain(i):
         e_copy(STEPS - 1, i).wait_send()
-        pl.when(r == 0)(lambda: e_copy(STEPS, i).wait_send())
         pl.when(has_front)(lambda: k_copy(STEPS - 1, 0, i).wait_send())
         pl.when(has_back)(lambda: k_copy(STEPS - 1, 1, i).wait_send())
     loop(CHUNKS, drain)
@@ -259,6 +318,7 @@
             pltpu.VMEM((2, J, I + 2, K, L), f32),
             pltpu.VMEM((2, I, K, L), f32),
             pltpu.VMEM((I, K, L), f32),
+            pltpu.VMEM((RELAYED, I // CHUNKS, K, L), f32),
             pltpu.VMEM((2, 2, J, I, L), f32),
             pltpu.VMEM((2, 2, J, I, L), f32),
             dma((3, CHUNKS)),
@@ -268,6 +328,9 @@
             dma((STEPS, 2)),
             dma((2, 2, CHUNKS)),
             dma((2, 2, CHUNKS)),
+            dma((RELAYED,)),
+            dma((RELAYED,)),
+            dma((RELAYED,)),
         ],
         compiler_params=pltpu.CompilerParams(
             collective_id=0, has_side_effects=True, vmem_limit_bytes=32 * 1024 * 1024),

time: 261 us -> 246 us (0.943)
  Pallas kernels: 260 us -> 246 us
    pallas_call x1, Pallas kernels: 254 us -> 239 us  [local(): pl.pallas_call(functools.partial(kernel, (J, I, K, L), sizes), out_shape=...]
where the time goes in v3:
time: 246 us
  Pallas kernels  246 us (100%)
    pallas_call x1, Pallas kernels, local(): pl.pallas_call(functools.partial(kernel, (J, I, K, L), sizes), out_shape=...  239 us
    pallas_call x1, Pallas kernels, local(): pl.pallas_call(write_out, out_shape=[jax.ShapeDtypeStruct((J, I, K, L), f...  6.08 us

profile of v3, /device:TPU:112, one launch (start us, length us, event | category | flops | bytes accessed | tf_op | source)
XLA Modules:
  0.0 246.2 jit_solution(10542763604799405621)
XLA Ops:
  0.6 239.5 %diffuse.1 = (f32[4,64,64,128]{3,2,1,0:T(8,128)S(1)}, f32[4,64,64,128]{3,2,1,0:T(8,128)S(1)}) custom-call(f32[4,64,64,128]{3,2,1,0:T(8,128)} %f_hbm.1, f32[4,64,64,128]{3,2,1,0:T(8,128)} %m_hbm.1, f32[4,64,64,128]{3,2,1,0:T(8,128)} %s_hbm.1), custom_call_target="tpu_custom_call" | custom-call | tf_op jit(solution)/shard_map/diffuse/pallas_call | solution.py:312
  240.1 6.1 %write_out.1 = (f32[4,64,64,128]{3,2,1,0:T(8,128)}, f32[4,64,64,128]{3,2,1,0:T(8,128)}) custom-call(f32[4,64,64,128]{3,2,1,0:T(8,128)S(1)} %get-tuple-element.4.cs_vmem, f32[4,64,64,128]{3,2,1,0:T(8,128)S(1)} %get-tuple-element.5.fe_vmem), custom_call_target="tpu_custom_call" | custom-call | tf_op jit(solution)/shard_map/write_out/pallas_call | solution.py:339

commit v4 on v3

--- a/solution.py
+++ b/solution.py
@@ -9,8 +9,8 @@
 
 STEPS = 4
 CHUNKS = 16
-FIRST = 6
-RELAYED = 6
+FIRST = 5
+RELAYED = 7
 MESH = pl.DeviceIdType.MESH
 
 
@@ -100,8 +100,6 @@
              + (s + n_slabs - 1) // n_slabs + (2 * n_slabs - 2 - s) // n_slabs)
     pl.semaphore_wait(barrier, peers)
 
-    pl.when(has_high)(lambda: h_copy(0, 1).start())
-    pl.when(has_low)(lambda: h_copy(0, 0).start())
     span(FIRST, CHUNKS, lambda i: e_copy(0, i).start())
     span(0, FIRST, lambda i: e_copy(0, i).start())
 
@@ -188,9 +186,8 @@
             loop(W, lambda i, p=p: stencil_row(
                 t, p, base + i, lambda row: F[now, p - 1, row + 1] + F[now, p + 1, row + 1]))
         if t < STEPS - 1:
-            if t > 0:
-                pl.when(first)(lambda: send_halo(t + 1, 0))
-                pl.when(last)(lambda: send_halo(t + 1, 1))
+            pl.when(first)(lambda: send_halo(t + 1, 0))
+            pl.when(last)(lambda: send_halo(t + 1, 1))
             send_faces(t + 1, chunk)
         else:
             @pl.when(r == 0)
@@ -227,26 +224,25 @@
         loop(2, lambda i: step_chunk(t, a + i * (CHUNKS - 1 - 2 * a), totals))
 
     for t in range(STEPS - 1):
-        span(FIRST, CHUNKS - t, lambda chunk: step_chunk(t, chunk))
-        span(t, FIRST, lambda chunk: step_chunk(t, chunk))
-    send_halo(1, 0)
-    send_halo(1, 1)
+        span(FIRST, CHUNKS - 1 - t, lambda chunk: step_chunk(t, chunk))
+        span(t + 1, FIRST, lambda chunk: step_chunk(t, chunk))
+    send_halo(0, 0)
+    send_halo(0, 1)
     t = STEPS - 1
     after = FIRST + RELAYED
     span(FIRST, after, lambda chunk: step_chunk(t, chunk, "relay"))
-    span(after, CHUNKS - t, lambda chunk: step_chunk(t, chunk))
-    span(t, FIRST, lambda chunk: step_chunk(t, chunk))
-    held = list(range(after, CHUNKS - t)) + list(range(t, FIRST))
-    both_ends(1, 0)
-    send_totals(*held[:2])
-    both_ends(2, 1)
-    both_ends(2, 0)
-    send_totals(*held[2:])
-    both_ends(3, 2, "direct")
-    hand_on(0, RELAYED // 2)
-    both_ends(3, 1, "direct")
-    both_ends(3, 0, "direct")
-    hand_on(RELAYED // 2, RELAYED)
+    span(after, CHUNKS - STEPS, lambda chunk: step_chunk(t, chunk))
+    span(STEPS, FIRST, lambda chunk: step_chunk(t, chunk))
+    held = list(range(after, CHUNKS - STEPS)) + list(range(STEPS, FIRST))
+    for begin in range(STEPS):
+        for t in range(begin, STEPS):
+            both_ends(t, t - begin, "direct")
+            if t == begin == 2:
+                send_totals(*held)
+            if (begin, t) == (1, 3):
+                hand_on(0, RELAYED // 2)
+            if (begin, t) == (2, 3):
+                hand_on(RELAYED // 2, RELAYED)
 
     @pl.when(r == 0)
     def _():
@@ -268,10 +264,10 @@
                     total = total + S[p, row]
                     M[p, row] = total * (1.0 / (J * n_rows))
             loop(W, sums)
-        span(after, CHUNKS - t, finish)
-        span(t, FIRST, finish)
-        for a in (2, 1):
+        for a in (3, 2, 1):
             loop(2, lambda i: finish(a + i * (CHUNKS - 1 - 2 * a)))
+        span(after, CHUNKS - STEPS, finish)
+        span(STEPS, FIRST, finish)
         span(FIRST, after, finish)
         loop(2, lambda i: finish(i * (CHUNKS - 1)))
         for i in range(RELAYED):

time: 246 us -> 244 us (level)
  Pallas kernels: 246 us -> 243 us
    pallas_call x1, Pallas kernels: 239 us -> 237 us  [local(): pl.pallas_call(functools.partial(kernel, (J, I, K, L), sizes), out_shape=...]
where the time goes in v4:
time: 244 us; the launch traced here: 243 us
  Pallas kernels  243 us (100%)
    pallas_call x1, Pallas kernels, local(): pl.pallas_call(functools.partial(kernel, (J, I, K, L), sizes), out_shape=...  237 us
    pallas_call x1, Pallas kernels, local(): pl.pallas_call(write_out, out_shape=[jax.ShapeDtypeStruct((J, I, K, L), f...  6.08 us

profile of v4, /device:TPU:112, one launch (start us, length us, event | category | flops | bytes accessed | tf_op | source)
XLA Modules:
  0.0 243.4 jit_solution(3001514249860912966)
XLA Ops:
  0.6 236.7 %diffuse.1 = (f32[4,64,64,128]{3,2,1,0:T(8,128)S(1)}, f32[4,64,64,128]{3,2,1,0:T(8,128)S(1)}) custom-call(f32[4,64,64,128]{3,2,1,0:T(8,128)} %f_hbm.1, f32[4,64,64,128]{3,2,1,0:T(8,128)} %m_hbm.1, f32[4,64,64,128]{3,2,1,0:T(8,128)} %s_hbm.1), custom_call_target="tpu_custom_call" | custom-call | tf_op jit(solution)/shard_map/diffuse/pallas_call | solution.py:308
  237.3 6.1 %write_out.1 = (f32[4,64,64,128]{3,2,1,0:T(8,128)}, f32[4,64,64,128]{3,2,1,0:T(8,128)}) custom-call(f32[4,64,64,128]{3,2,1,0:T(8,128)S(1)} %get-tuple-element.4.cs_vmem, f32[4,64,64,128]{3,2,1,0:T(8,128)S(1)} %get-tuple-element.5.fe_vmem), custom_call_target="tpu_custom_call" | custom-call | tf_op jit(solution)/shard_map/write_out/pallas_call | solution.py:335

commit v5 on v4

--- a/solution.py
+++ b/solution.py
@@ -284,19 +284,18 @@
 
 
 def write_out(cs_vmem, fe_vmem, cs_hbm, fe_hbm, sem):
-    W = cs_vmem.shape[1] // CHUNKS
-
-    def put(which, i):
+    J, W = cs_vmem.shape[0], cs_vmem.shape[1] // CHUNKS
+
+    def put(which, p, i):
         src, dst = ((cs_vmem, cs_hbm), (fe_vmem, fe_hbm))[which]
         rows = pl.ds(i * W, W)
-        return pltpu.make_async_copy(src.at[:, rows], dst.at[:, rows], sem.at[which, i])
-
-    for i in range(CHUNKS):
-        put(0, i).start()
-        put(1, i).start()
-    for i in range(CHUNKS):
-        put(0, i).wait()
-        put(1, i).wait()
+        return pltpu.make_async_copy(src.at[p, rows], dst.at[p, rows], sem.at[which, p, i])
+
+    pieces = [(which, p, i) for which in range(2) for p in range(J) for i in range(CHUNKS)]
+    for piece in pieces:
+        put(*piece).start()
+    for piece in pieces:
+        put(*piece).wait()
 
 
 def local(sizes, field_values, mobility, source):
@@ -337,7 +336,7 @@
         out_shape=[jax.ShapeDtypeStruct((J, I, K, L), f32)] * 2,
         in_specs=[vmem] * 2,
         out_specs=[any_space] * 2,
-        scratch_shapes=[dma((2, CHUNKS))],
+        scratch_shapes=[dma((2, J, CHUNKS))],
         compiler_params=pltpu.CompilerParams(vmem_limit_bytes=1024 * 1024),
         name="write_out",
     )(column_sum, field_end))

time: 244 us -> 244 us (level)
  no operation moved by 1% of the time
where the time goes in v5:
time: 244 us
  Pallas kernels  244 us (100%)
    pallas_call x1, Pallas kernels, local(): pl.pallas_call(functools.partial(kernel, (J, I, K, L), sizes), out_shape=...  237 us
    pallas_call x1, Pallas kernels, local(): pl.pallas_call(write_out, out_shape=[jax.ShapeDtypeStruct((J, I, K, L), f...  6.87 us

profile of v5, /device:TPU:112, one launch (start us, length us, event | category | flops | bytes accessed | tf_op | source)
XLA Modules:
  0.0 244.2 jit_solution(1802257889407353185)
XLA Ops:
  0.6 236.7 %diffuse.1 = (f32[4,64,64,128]{3,2,1,0:T(8,128)S(1)}, f32[4,64,64,128]{3,2,1,0:T(8,128)S(1)}) custom-call(f32[4,64,64,128]{3,2,1,0:T(8,128)} %f_hbm.1, f32[4,64,64,128]{3,2,1,0:T(8,128)} %m_hbm.1, f32[4,64,64,128]{3,2,1,0:T(8,128)} %s_hbm.1), custom_call_target="tpu_custom_call" | custom-call | tf_op jit(solution)/shard_map/diffuse/pallas_call | solution.py:307
  237.3 6.9 %write_out.1 = (f32[4,64,64,128]{3,2,1,0:T(8,128)}, f32[4,64,64,128]{3,2,1,0:T(8,128)}) custom-call(f32[4,64,64,128]{3,2,1,0:T(8,128)S(1)} %get-tuple-element.4.cs_vmem, f32[4,64,64,128]{3,2,1,0:T(8,128)S(1)} %get-tuple-element.5.fe_vmem), custom_call_target="tpu_custom_call" | custom-call | tf_op jit(solution)/shard_map/write_out/pallas_call | solution.py:334
